TPU v7x, 256 devices: a whole 4x4x8 slice. The times are simulated.
256 devices in a mesh: wave: 32 (over x, z_hi, core), level: 8 (over y, z_lo).
Axes of the slice: x: 4, y: 4, z: 8 (z_hi: 4, z_lo: 2; z = z_hi * 2 + z_lo), core: 2. Of those that a mesh axis runs over, the one named last changes fastest.
Arguments:
- state: float32 [4, 64, 256, 2, 256], P(None, 'level', 'wave'), may hold values from -0.02 to 0.02
- legendre: float32 [256, 384, 256], P('wave'), may hold values from -6 to 6
- lat_weight: float32 [384], P('wave'), may hold values from 0.8 to 2
- modes: float32 [64, 64], replicated, may hold values from -1 to 1, as said below
- mode_rates: float32 [64], replicated, may hold values from 1e-05 to 0.003
- diffusion: float32 [4], replicated, may hold values from 0.3 to 3
- norm_gain: float32 [256], replicated, may hold values from 0.5 to 1.5
- w_first: bfloat16 [1024, 256], replicated, may hold values from -0.375 to 0.375
- b_first: float32 [1024], replicated, may hold values from -3 to 3
- w_second: bfloat16 [1024, 1024], replicated, may hold values from -0.1875 to 0.1875
- b_second: float32 [1024], replicated, may hold values from -3 to 3
- w_third: bfloat16 [256, 1024], replicated, may hold values from -0.1875 to 0.1875
- b_third: float32 [256], replicated, may hold values from -1.2 to 1.2
Outputs:
- next_state: float32 [4, 64, 256, 2, 256], P(None, 'level', 'wave')
Inputs may be any that keep to these rules, and one draw needn't show every extreme that they name: `modes`: orthogonal: its transpose is its inverse.
All inputs are finite; a program needn't handle non-finite values.
Results may differ from a plain program's by a relative error of at most 0.0011.
Values may be sent and summed in bfloat16 or wider, within the bound.
A program may use at most 128 MiB of HBM per device.

v0:
```python
import jax
import jax.numpy as jnp
import numpy as np
from jax import lax
from jax.experimental import pallas as pl
from jax.experimental.pallas import tpu as pltpu
from jax.sharding import PartitionSpec as P

F, LEV, M, LAT, LON, HID = 4, 64, 256, 384, 768, 1024
HALF = LON // 2
EPS = 1e-06
LOGICAL = pl.DeviceIdType.LOGICAL
bf16, f32 = jnp.bfloat16, jnp.float32


def tables():
    b = np.arange(4)[:, None]
    r = np.arange(128)[None, :]
    m = (8 * (r // 4) + 2 * (r % 4) + b // 2).reshape(-1)
    c = np.broadcast_to(b % 2, (4, 128)).reshape(-1)
    o = np.arange(HALF)
    angle = 2.0 * np.pi * ((m[:, None] * o[None, :]) % LON) / LON
    wave = np.where(c[:, None] == 0, np.cos(angle), -np.sin(angle))
    inverse = (np.where(m == 0, 1.0, 2.0)[:, None] * wave).T.astype(np.float32)
    forward = (wave / LON).astype(np.float32)
    parts = []
    for t in (inverse, forward):
        hi = t.astype(jnp.bfloat16)
        parts += [hi, (t - hi.astype(np.float32)).astype(jnp.bfloat16)]
    return parts


def split(x):
    hi = x.astype(bf16)
    return hi, (x - hi.astype(f32)).astype(bf16)


def encode(x):
    hi = x.astype(bf16).astype(f32)
    size = jnp.abs(hi)
    r = jnp.where(size > 0.0, (x - hi) / size, 0.0)
    return hi, jnp.clip(jnp.floor(r * 2048.0 + 8.0), 0.0, 15.0)


def decode(hi, k):
    return hi + jnp.abs(hi) * ((k - 7.5) * (1.0 / 2048.0))


def gelu(x):
    c = 0.7978845608028654
    half = 0.5 * x
    return half + half * jnp.tanh(x * (c + (c * 0.044715) * (x * x)))


def nn(a, b):
    return lax.dot_general(a, b, (((1,), (0,)), ((), ())), preferred_element_type=f32)


def nt(a, b):
    return lax.dot_general(a, b, (((1,), (1,)), ((), ())), preferred_element_type=f32)


def block_transpose(v):
    lane = lax.broadcasted_iota(jnp.int32, v[0].shape, 1)
    low, even = lane < 64, (lane % 64) < 32
    l02 = jnp.where(low, v[0], pltpu.roll(v[2], 64, 1))
    h02 = jnp.where(low, pltpu.roll(v[0], 64, 1), v[2])
    l13 = jnp.where(low, v[1], pltpu.roll(v[3], 64, 1))
    h13 = jnp.where(low, pltpu.roll(v[1], 64, 1), v[3])
    return [
        jnp.where(even, l02, pltpu.roll(l13, 32, 1)),
        jnp.where(even, pltpu.roll(l02, 96, 1), l13),
        jnp.where(even, h02, pltpu.roll(h13, 32, 1)),
        jnp.where(even, pltpu.roll(h02, 96, 1), h13),
    ]


class Place:
    def __init__(self):
        self.w, self.i = lax.axis_index("wave"), lax.axis_index("level")
        w, i = self.w, self.i
        self.p, self.core, self.y, self.zl = w // 2, w % 2, i // 2, i % 2
        x, z = w // 8, ((w // 2) % 4) * 2 + i % 2
        self.xs = [(x + d) % 4 for d in range(4)]
        self.zs = [(z + d) % 8 for d in range(8)]
        self.ys = [(self.y + d) % 4 for d in range(4)]

    def plane(self):
        for dz in (4, 3, 5, 2, 6, 1, 7, 0):
            for dx in (2, 1, 3, 0):
                zh, zl = self.zs[dz] // 2, self.zs[dz] % 2
                p = self.xs[dx] * 4 + zh
                for core in (0, 1):
                    yield dz == 0 and dx == 0, core, p, zl, p * 16 + core * 8 + self.y * 2 + zl

    def level(self):
        for d in (4, 2, 6, 3, 5, 1, 7):
            i = (self.i + d) % 8
            yield d, i, self.w * 8 + i

    def column(self):
        for d in (2, 1, 3):
            yield d, self.ys[d], self.w * 8 + self.ys[d] * 2 + self.zl


def remote(src, dst, send, recv, device):
    return pltpu.make_async_remote_copy(src, dst, send, recv, device_id=device, device_id_type=LOGICAL)


def meet(at):
    barrier = pltpu.get_barrier_semaphore()
    for d, i, device in at.level():
        pl.semaphore_signal(barrier, inc=1, device_id=device, device_id_type=LOGICAL)
    buddy = (at.w + 1 - 2 * at.core) * 8 + at.i
    pl.semaphore_signal(barrier, inc=1, device_id=buddy, device_id_type=LOGICAL)
    for dz in (4, 3, 5, 2, 6, 1, 7, 0):
        for dx in (2, 1, 3, 0):
            if dz == 0 and dx == 0:
                continue
            zh, zl = at.zs[dz] // 2, at.zs[dz] % 2
            for core in (0, 1):
                device = ((at.xs[dx] * 4 + zh) * 2 + core) * 8 + at.y * 2 + zl
                pl.semaphore_signal(barrier, inc=1, device_id=device, device_id_type=LOGICAL)
    return barrier, 7 + 1 + 62 + 0


def legendre_forward(at, r):
    w = at.w
    col = lax.broadcasted_iota(jnp.int32, (64, M), 1)

    def pair(q, carry):
        acc = jnp.zeros((LAT, 128), f32)
        for h in range(2):
            m = 2 * q + h
            s = jnp.concatenate([r.state[:, :, m, c, :].reshape(32, M) for c in range(2)], axis=0)
            s = jnp.where(col < M - (8 * w + m), s, 0.0)
            hi, lo = split(s)
            zero = jnp.zeros_like(hi)
            order = (hi, zero, lo, zero) if h == 0 else (zero, hi, zero, lo)
            right = jnp.concatenate(order, axis=0)
            pltpu.make_async_copy(r.leg.at[m], r.leg_v.at[m], r.leg_sem.at[m]).wait()
            bhi, blo = split(r.leg_v[m])
            r.leg_hi[m] = bhi
            r.leg_lo[m] = blo
            both = nt(bhi, right)
            acc += both[:, :128] + both[:, 128:] + nt(blo, right[:128])
        r.band[q] = acc
        return carry

    lax.fori_loop(0, 4, pair, 0)

    def pack(k, carry):
        code = []
        for q in range(4):
            hi, step = encode(r.band[q, pl.ds(pl.multiple_of(24 * k, 8), 24), :])
            r.tmp[pl.ds(q, 24, stride=4), :] = hi
            code.append(step)
        r.tmc[pl.ds(0, 24, stride=2), :] = 16.0 * code[0] + code[1]
        r.tmc[pl.ds(1, 24, stride=2), :] = 16.0 * code[2] + code[3]
        hi = r.tmp[...].reshape(4, 2, 3, 4, 128).astype(bf16)
        low = r.tmc[...].reshape(4, 2, 3, 2, 128).astype(bf16)
        for t in range(3):
            r.pa[t, :, pl.ds(2 * k, 2)] = hi[:, :, t]
            r.ca[t, :, pl.ds(2 * k, 2)] = low[:, :, t]
        return carry

    lax.fori_loop(0, 16, pack, 0)


def along_y_start(at, t, pairs, send, recv, own_sem):
    for n, (src, dst) in enumerate(pairs):
        for d, y, device in at.column():
            remote(src.at[t, y], dst.at[t, at.y], send.at[n, t], recv.at[n, t], device).start()
        pltpu.make_async_copy(src.at[t, at.y], dst.at[t, at.y], own_sem.at[n, t]).start()


def along_y_wait(at, t, pairs, send, recv, own_sem):
    for n, (src, dst) in enumerate(pairs):
        remote(src.at[t, pl.ds(0, 3)], dst.at[t, pl.ds(0, 3)], send.at[n, t], recv.at[n, t], 0).wait()
        pltpu.make_async_copy(src.at[t, at.y], dst.at[t, at.y], own_sem.at[n, t]).wait()


def to_grid_start(at, r, t):
    core, a = (0, t) if t < 2 else (1, 0)
    me = at.w * 2 + at.zl
    for n, (src, dst) in enumerate(((r.r1, r.xh), (r.c1, r.xc))):
        for chip, pc, p, zl, device in at.plane():
            if pc != core:
                continue
            piece, goal = src.at[t, :, p * 2 + zl], dst.at[a, me]
            copy = remote(piece, goal, r.s2.at[n, t], r.v2.at[n, a], device)
            if chip:
                pl.when(at.core != core)(lambda copy=copy: copy.start())
            else:
                copy.start()
        own = pltpu.make_async_copy(src.at[t, :, at.p * 2 + at.zl], dst.at[a, me], r.own_sem.at[n, a])
        pl.when(at.core == core)(lambda own=own: own.start())


def to_grid_arrived(at, r, a):
    me = at.w * 2 + at.zl
    for n, (src, dst) in enumerate(((r.r1, r.xh), (r.c1, r.xc))):
        some = dst.at[a, pl.ds(0, 63)]
        remote(some, some, r.s2.at[n, 0], r.v2.at[n, a], 0).wait_recv()
        pltpu.make_async_copy(src.at[0, :, 0], dst.at[a, me], r.own_sem.at[n, a]).wait()


def to_grid_sent(at, r, t):
    for n, src in enumerate((r.r1, r.c1)):
        for core in range(2):
            pieces = 31 if core == (0 if t < 2 else 1) else 32

            @pl.when(at.core == core)
            def _(n=n, src=src, pieces=pieces):
                some = src.at[t, :, pl.ds(0, pieces)]
                remote(some, some, r.s2.at[n, t], r.v2.at[n, 0], 0).wait_send()


def one_latitude(at, r, a):
    e = 3 * at.i + (a if a else jnp.where(at.core == 0, 0, 2))
    lane12 = lax.broadcasted_iota(jnp.int32, (2, 1, 128), 2)
    number = lax.broadcasted_iota(jnp.int32, (2, 1, 128), 0) * 12 + lane12
    weight = jnp.sum(jnp.where((number == e) & (lane12 < 12), r.lat[...], 0.0))
    for g in range(2):
        v = []
        for k in range(4):
            y, zl = 2 * g + k // 2, k % 2
            code = r.xc.reshape(2, 32, 2, 4, 2, 128)[a, :, zl, y].astype(f32).reshape(64, 128)
            first = jnp.floor(code * (1.0 / 16.0))
            r.steps[k, pl.ds(0, 64, stride=2), :] = first
            r.steps[k, pl.ds(1, 64, stride=2), :] = code - 16.0 * first
            v.append(decode(r.xh.reshape(2, 32, 2, 4, 4, 128)[a, :, zl, y].astype(f32).reshape(128, 128), r.steps[k]))
        for b, t in enumerate(block_transpose(v)):
            here = (slice(b * 128, (b + 1) * 128), slice(g * 128, (g + 1) * 128))
            r.xt[here], r.xl[here] = split(t)

    def inverse(rows, half):
        hi, lo, x, rest = r.ih[rows, half], r.il[rows, half], r.xt[half, :], r.xl[half, :]
        return nn(hi, x) + nn(lo, x) + nn(hi, rest)

    def columns(k, carry):
        rows = pl.ds(pl.multiple_of(k * 128, 128), 128)
        even, odd = inverse(rows, slice(0, 256)), inverse(rows, slice(256, 512))
        grid = jnp.concatenate([even + odd, even - odd], axis=0)
        v = grid.astype(bf16).astype(f32)
        scale = lax.rsqrt(jnp.mean(v * v, axis=1, keepdims=True) + EPS)
        n = (v * scale * r.gain_p[...]).astype(bf16)
        h = gelu(nt(n, r.w1p[...]) + r.b1[...]).astype(bf16)
        h = gelu(nt(h, r.w2v[...]) + r.b2[...]).astype(bf16)
        t = (nt(h, r.w3p[...]) + r.b3p[...]).astype(bf16)
        u = (grid + t.astype(f32)) * weight
        r.s_hi[rows, :], r.s_lo[rows, :] = split(u[:128] + u[128:])
        r.d_hi[rows, :], r.d_lo[rows, :] = split(u[:128] - u[128:])
        return carry

    lax.fori_loop(0, 3, columns, 0)

    def forward(half, hi, lo):
        return nn(r.fh[half, :], hi[...]) + nn(r.fh[half, :], lo[...]) + nn(r.fl[half, :], hi[...])

    even, odd = forward(slice(0, 256), r.s_hi, r.s_lo), forward(slice(256, 512), r.d_hi, r.d_lo)
    y = (even[:128], even[128:], odd[:128], odd[128:])
    for g in range(2):
        for k, t in enumerate(block_transpose([v[:, g * 128 : (g + 1) * 128] for v in y])):
            hi, step = encode(t)
            r.steps[k] = step
            code = 16.0 * r.steps[k, pl.ds(0, 64, stride=2), :] + r.steps[k, pl.ds(1, 64, stride=2), :]
            r.yh.reshape(2, 32, 2, 4, 4, 128)[a, :, k % 2, 2 * g + k // 2] = hi.reshape(32, 4, 128).astype(bf16)
            r.yc.reshape(2, 32, 2, 4, 2, 128)[a, :, k % 2, 2 * g + k // 2] = code.reshape(32, 2, 128).astype(bf16)


def network_weights(r):
    row = lax.broadcasted_iota(jnp.int32, (256, 256), 0)
    lane = lax.broadcasted_iota(jnp.int32, (256, 256), 1)
    pick = row == ((lane // 8) % 4) * 64 + (lane // 32) * 8 + lane % 8
    r.w1p[...] = nn(r.w1v[...], pick.astype(bf16)).astype(bf16)
    for k in range(8):
        for f in range(4):
            r.w3p[k * 32 + f * 8 : k * 32 + f * 8 + 8, :] = r.w3v[f * 64 + k * 8 : f * 64 + k * 8 + 8, :]
    for a, b in ((r.gain, r.gain_p), (r.b3, r.b3p)):
        rows = jnp.broadcast_to(a[...], (8, 256))
        b[...] = jnp.dot(rows, pick.astype(f32), precision=lax.Precision.HIGHEST, preferred_element_type=f32)[:1]


def send_latitude(at, r, a, mc):
    t = a if mc == 0 else 2
    me = at.p * 2 + at.zl
    for n, (src, dst) in enumerate(((r.yh, r.r2), (r.yc, r.c2))):
        for chip, core, p, zl, device in at.plane():
            if not (chip and core == mc):
                piece = src.at[a, (p * 2 + core) * 2 + zl]
                remote(piece, dst.at[t, :, me], r.s3.at[n, a], r.v3.at[n, t], device).start()
        pltpu.make_async_copy(src.at[a, at.w * 2 + at.zl], dst.at[t, :, me], r.own_sem.at[n, a]).start()


def latitude_own(at, r, a):
    for n, (src, dst) in enumerate(((r.yh, r.r2), (r.yc, r.c2))):
        pltpu.make_async_copy(src.at[a, 0], dst.at[0, :, 0], r.own_sem.at[n, a]).wait()


def latitude_sent(at, r, a):
    for n, src in enumerate((r.yh, r.yc)):
        some = src.at[a, pl.ds(0, 63)]
        remote(some, some, r.s3.at[n, a], r.v3.at[n, 0], 0).wait_send()


def wait_latitude(at, r, t):
    for n, dst in enumerate((r.r2, r.c2)):
        for core in range(2):
            pieces = 31 if core == (0 if t < 2 else 1) else 32

            @pl.when(at.core == core)
            def _(n=n, dst=dst, pieces=pieces):
                some = dst.at[t, :, pl.ds(0, pieces)]
                remote(some, some, r.s3.at[n, 0], r.v3.at[n, t], 0).wait_recv()


def legendre_back(at, r):
    def unpack(k, carry):
        hi = jnp.stack([r.vr[t, :, pl.ds(2 * k, 2)].astype(f32) for t in range(3)], axis=2)
        low = jnp.stack([r.vc[t, :, pl.ds(2 * k, 2)].astype(f32) for t in range(3)], axis=2)
        r.vs[pl.ds(pl.multiple_of(96 * k, 8), 96), :] = hi.reshape(96, 128)
        r.vcs[pl.ds(pl.multiple_of(48 * k, 8), 48), :] = low.reshape(48, 128)
        return carry

    lax.fori_loop(0, 16, unpack, 0)
    for q in range(4):
        code = r.vcs[pl.ds(q // 2, LAT, stride=2), :]
        first = jnp.floor(code * (1.0 / 16.0))
        step = first if q % 2 == 0 else code - 16.0 * first
        turned = decode(r.vs[pl.ds(q, LAT, stride=4), :], step).T
        r.vt[q], r.vl[q] = split(turned)
        for h in range(2):
            one = jnp.concatenate([turned[h * 64 + c * 32 + 8 : h * 64 + c * 32 + 16] for c in range(2)], axis=0)
            r.v1t[2 * q + h], r.v1l[2 * q + h] = split(one)
    col = lax.broadcasted_iota(jnp.int32, (64, M), 1)
    field = (lax.broadcasted_iota(jnp.int32, (64, M), 0) // 8) % 4
    strength = jnp.where(
        field == 0, r.diff[0], jnp.where(field == 1, r.diff[1], jnp.where(field == 2, r.diff[2], r.diff[3]))
    )

    def damping(n, strength):
        g = (n * (n + 1)).astype(f32) / (M * (M - 1))
        return 1.0 + strength * (g * g)

    def level_rows(ref, i):
        return ref.at[:, pl.ds(pl.multiple_of(8 * i, 8), 8), :]

    def basis(left, rest, m):
        n = 8 * at.w + m + col[: left.shape[0]]
        spec = nn(left, r.leg_hi[m]) + nn(left, r.leg_lo[m]) + nn(rest, r.leg_hi[m])
        return n, jnp.where(n < M, spec, 0.0)

    def field_one(m, carry):
        n, spec = basis(r.v1t[m], r.v1l[m], m)
        for c in range(2):
            r.f1[m, c] = spec[c * 8 : c * 8 + 8]
        return carry

    lax.fori_loop(0, 8, field_one, 0)
    for d, i, device in at.level():
        remote(r.f1.at[i], level_rows(r.g1, at.i), r.s5, r.v5, device).start()
    own = pltpu.make_async_copy(r.f1.at[at.i], level_rows(r.g1, at.i), r.own_sem.at[0, 0])
    own.start()

    def pair(q, carry):
        for h in range(2):
            m = 2 * q + h
            n, spec = basis(r.vt[q, h * 64 : (h + 1) * 64, :], r.vl[q, h * 64 : (h + 1) * 64, :], m)
            done = spec / damping(n, strength)
            for c in range(2):
                r.out[:, :, m, c, :] = done[c * 32 : (c + 1) * 32].reshape(F, 8, M)
        return carry

    lax.fori_loop(0, 4, pair, 0)
    own.wait()
    n = 8 * at.w + at.i + col
    row = lax.broadcasted_iota(jnp.int32, (64, 64), 0)
    lane = lax.broadcasted_iota(jnp.int32, (64, 64), 1)
    rates = jnp.sum(jnp.where(row == lane, r.rates[...], 0.0), axis=1, keepdims=True)
    divisor = 1.0 + rates * (n * (n + 1)).astype(f32)
    damp = damping(n, r.diff[1])
    remote(r.f1.at[pl.ds(0, 7)], r.g1.at[:, pl.ds(0, 56), :], r.s5, r.v5, 0).wait_recv()
    for c in range(2):
        amplitude = lax.dot_general(
            r.modes[...], r.g1[c], (((0,), (0,)), ((), ())), precision=lax.Precision.HIGHEST, preferred_element_type=f32
        )
        solved = jnp.dot(
            r.modes[...], amplitude / divisor, precision=lax.Precision.HIGHEST, preferred_element_type=f32
        )
        r.hs[c] = solved / damp
    for d, i, device in at.level():
        remote(level_rows(r.hs, i), r.qs.at[at.i], r.s6, r.v6, device).start()
    own = pltpu.make_async_copy(level_rows(r.hs, at.i), r.qs.at[at.i], r.own_sem.at[1, 0])
    own.start()
    own.wait()
    remote(r.f1.at[pl.ds(0, 7)], r.g1.at[:, pl.ds(0, 56), :], r.s5, r.v5, 0).wait_send()
    remote(r.hs.at[:, pl.ds(0, 56), :], r.qs.at[pl.ds(0, 7)], r.s6, r.v6, 0).wait()
    for m in range(8):
        for c in range(2):
            r.out[1, :, m, c, :] = r.qs[m, c]


INPUTS = ["state_in", "leg", "lw", "modes", "rates", "diff", "gain", "w1", "b1", "w2", "b2", "w3", "b3", "ihh", "ilh", "fhh", "flh"]
DMA = pltpu.SemaphoreType.DMA
SCRATCH = dict(
    state=((F, 8, 8, 2, M), f32), leg_v=((8, LAT, M), f32), leg_hi=((8, LAT, M), bf16), leg_lo=((8, LAT, M), bf16), band=((4, LAT, 128), f32),
    tmp=((96, 128), f32), tmc=((48, 128), f32), pa=((3, 4, 32, 4, 128), bf16), ca=((3, 4, 32, 2, 128), bf16),
    r1=((3, 4, 32, 4, 128), bf16), c1=((3, 4, 32, 2, 128), bf16), xh=((2, 64, 4, 4, 128), bf16),
    xc=((2, 64, 4, 2, 128), bf16), lat=((2, 1, 128), f32), row=((1, 128), f32), w1v=((HID, 256), bf16),
    w2v=((HID, HID), bf16), w3v=((256, HID), bf16), ih=((HALF, 512), bf16), il=((HALF, 512), bf16),
    fh=((512, HALF), bf16), fl=((512, HALF), bf16), w1p=((HID, 256), bf16), w3p=((256, HID), bf16),
    gain_p=((1, 256), f32), b3p=((1, 256), f32), steps=((4, 128, 128), f32), xt=((512, 256), bf16),
    xl=((512, 256), bf16), s_hi=((HALF, 256), bf16), s_lo=((HALF, 256), bf16), d_hi=((HALF, 256), bf16),
    d_lo=((HALF, 256), bf16), yh=((2, 64, 4, 4, 128), bf16), yc=((2, 64, 4, 2, 128), bf16),
    r2=((3, 4, 32, 4, 128), bf16), c2=((3, 4, 32, 2, 128), bf16), vr=((3, 4, 32, 4, 128), bf16),
    vc=((3, 4, 32, 2, 128), bf16), vs=((1536, 128), f32), vcs=((768, 128), f32), vt=((4, 128, LAT), bf16),
    vl=((4, 128, LAT), bf16), f1=((8, 2, 8, M), f32), g1=((2, 64, M), f32), hs=((2, 64, M), f32),
    qs=((8, 2, 8, M), f32), v1t=((8, 16, LAT), bf16), v1l=((8, 16, LAT), bf16),
)
SEMS = dict(
    leg_sem=(8,), load_sem=(8,), own_sem=(2, 2), lat_sem=(3,), y_own=(2, 3), s1=(2, 3), v1=(2, 3), s2=(2, 3), v2=(2, 2),
    s3=(2, 2), v3=(2, 3), s4=(2, 3), v4=(2, 3), s5=(), v5=(), s6=(), v6=(),
)


class Refs:
    pass


def step_kernel(*refs):
    r = Refs()
    for name, ref in zip(INPUTS + ["out"] + list(SCRATCH) + list(SEMS), refs, strict=True):
        setattr(r, name, ref)
    at = Place()
    whole_state = pltpu.make_async_copy(r.state_in, r.state, r.load_sem.at[7])
    whole_state.start()
    pltpu.make_async_copy(r.leg.at[0], r.leg_v.at[0], r.leg_sem.at[0]).start()
    barrier, callers = meet(at)
    for m in range(1, 8):
        pltpu.make_async_copy(r.leg.at[m], r.leg_v.at[m], r.leg_sem.at[m]).start()
    loads = [
        pltpu.make_async_copy(a, b, r.load_sem.at[n])
        for n, (a, b) in enumerate(
            ((r.w1, r.w1v), (r.w3, r.w3v), (r.w2, r.w2v), (r.ihh, r.ih), (r.ilh, r.il), (r.fhh, r.fh), (r.flh, r.fl))
        )
    ]
    for load in loads:
        load.start()
    lane = lax.broadcasted_iota(jnp.int32, (1, 128), 1)
    row = jnp.zeros((1, 128), f32)
    for k in range(12):
        row = jnp.where(lane == k, r.lw[k], row)
    r.row[...] = row
    whole_state.wait()
    with jax.named_scope('legfwd'):
        legendre_forward(at, r)
    with jax.named_scope('barwait'):
        pl.semaphore_wait(barrier, callers)
    weights = remote(r.row, r.lat.at[at.core], r.lat_sem.at[0], r.lat_sem.at[1], (at.w + 1 - 2 * at.core) * 8 + at.i)
    weights.start()
    own = pltpu.make_async_copy(r.row, r.lat.at[at.core], r.lat_sem.at[2])
    own.start()
    sc = jax.named_scope
    order = (0, 2, 1)
    there = (((r.pa, r.r1), (r.ca, r.c1)), r.s1, r.v1, r.y_own)
    back = (((r.r2, r.vr), (r.c2, r.vc)), r.s4, r.v4, r.y_own)
    with sc("y1"):
        for t in order:
            along_y_start(at, t, *there)
        for t in order:
            along_y_wait(at, t, *there)
            to_grid_start(at, r, t)
    with sc("weights"):
        own.wait()
        weights.wait()
        for load in loads:
            load.wait()
        network_weights(r)
    with sc("arrive0"):
        to_grid_arrived(at, r, 0)
    with sc("lat0"):
        one_latitude(at, r, 0)

    @pl.when(at.core == 0)
    def _():
        with sc("send0"):
            send_latitude(at, r, 0, 0)
        with sc("arrive1"):
            to_grid_arrived(at, r, 1)
        with sc("lat1"):
            one_latitude(at, r, 1)
        with sc("send1"):
            send_latitude(at, r, 1, 0)
            latitude_own(at, r, 0)
            latitude_own(at, r, 1)

    @pl.when(at.core == 1)
    def _():
        with sc("send"):
            send_latitude(at, r, 0, 1)
            latitude_own(at, r, 0)

    with sc("y2"):
        for t in order:
            wait_latitude(at, r, t)
            along_y_start(at, t, *back)
        for t in order:
            along_y_wait(at, t, *back)
    with sc("legback"):
        legendre_back(at, r)
    with sc("sent"):
        for t in order:
            to_grid_sent(at, r, t)
        latitude_sent(at, r, 0)
        pl.when(at.core == 0)(lambda: latitude_sent(at, r, 1))


VMEM = pl.BlockSpec(memory_space=pltpu.VMEM)
SMEM = pl.BlockSpec(memory_space=pltpu.SMEM)
ANY = pl.BlockSpec(memory_space=pl.ANY)


def body(state, legendre, lat_weight, modes, mode_rates, diffusion, norm_gain, w_first, b_first, w_second, b_second, w_third, b_third):
    return pl.pallas_call(
        step_kernel,
        name="step",
        out_shape=jax.ShapeDtypeStruct((F, 8, 8, 2, M), f32),
        in_specs=[ANY, ANY, SMEM, VMEM, VMEM, SMEM, VMEM, ANY, VMEM, ANY, VMEM, ANY, VMEM, ANY, ANY, ANY, ANY],
        out_specs=VMEM,
        scratch_shapes=[pltpu.VMEM(*s) for s in SCRATCH.values()] + [DMA(s) if s else DMA for s in SEMS.values()],
        compiler_params=pltpu.CompilerParams(collective_id=0, has_side_effects=True),
    )(
        state, legendre, lat_weight, modes, mode_rates.reshape(1, LEV), diffusion, norm_gain.reshape(1, 256), w_first,
        b_first.reshape(1, HID), w_second, b_second.reshape(1, HID), w_third, b_third.reshape(1, 256),
        *[jnp.asarray(t) for t in tables()],
    )


def solution(mesh):
    return jax.shard_map(
        body,
        mesh=mesh,
        in_specs=(P(None, "level", "wave", None, None), P("wave", None, None), P("wave")) + (P(),) * 10,
        out_specs=P(None, "level", "wave", None, None),
        check_vma=False,
    )
```

profile of v0, /device:TPU:2, one launch (start us, length us, event | category | flops | bytes accessed | tf_op | source)
XLA Modules:
  0.0 68.1 jit_solution(123530043721349478)
XLA Ops:
  0.0 66.0 %step.1 = f32[4,8,8,2,256]{4,3,2,1,0:T(2,128)} custom-call(f32[4,8,8,2,256]{4,3,2,1,0:T(2,128)} %refs_0_.1, f32[8,384,256]{2,1,0:T(8,128)} %refs_1_.1, f32[12]{0:T(128)} %refs_2_.1, f32[64,64]{1,0:T(8,128)} %refs_3_.1, f32[1,64]{1,0:T(1,128)} %bitcast.9, f32[4]{0:T(128)} %refs_5_.1, f32[1,256]{1,0:T(1,128)} %bitcast.7, bf16[1024,256]{1,0:T(8,128)(2,1)} %refs_7_.1, ...), custom_call_target="tpu_custom_call" | custom-call | tf_op jit(solution)/shard_map/step/pallas_call | solution.py:525
  66.0 2.0 %copy.19 = f32[4,8,8,2,256]{4,3,2,1,0:T(2,128)} copy(f32[4,8,8,2,256]{4,3,2,1,0:T(2,128)} %step.1) | data formatting | bytes 1048576
where the time goes:
time: 68.3 us; the launch traced here: 68.1 us
  Pallas kernels  66 us (97%)
  local copies, waits for them, and re-layouts  2.02 us (3%)
    pallas_call x1, Pallas kernels, body(): pl.pallas_call(step_kernel, name='step', out_shape=jax.ShapeDtypeStruct((...  66 us
    unnamed x1, local copies, waits for them, and re-layouts  2.02 us

commit v1 on v0

--- a/solution.py
+++ b/solution.py
@@ -329,10 +329,8 @@
         first = jnp.floor(code * (1.0 / 16.0))
         step = first if q % 2 == 0 else code - 16.0 * first
         turned = decode(r.vs[pl.ds(q, LAT, stride=4), :], step).T
-        r.vt[q], r.vl[q] = split(turned)
         for h in range(2):
-            one = jnp.concatenate([turned[h * 64 + c * 32 + 8 : h * 64 + c * 32 + 16] for c in range(2)], axis=0)
-            r.v1t[2 * q + h], r.v1l[2 * q + h] = split(one)
+            r.vt[2 * q + h], r.vl[2 * q + h] = split(turned[h * 64 : (h + 1) * 64])
     col = lax.broadcasted_iota(jnp.int32, (64, M), 1)
     field = (lax.broadcasted_iota(jnp.int32, (64, M), 0) // 8) % 4
     strength = jnp.where(
@@ -346,33 +344,25 @@
     def level_rows(ref, i):
         return ref.at[:, pl.ds(pl.multiple_of(8 * i, 8), 8), :]
 
-    def basis(left, rest, m):
-        n = 8 * at.w + m + col[: left.shape[0]]
-        spec = nn(left, r.leg_hi[m]) + nn(left, r.leg_lo[m]) + nn(rest, r.leg_hi[m])
-        return n, jnp.where(n < M, spec, 0.0)
-
-    def field_one(m, carry):
-        n, spec = basis(r.v1t[m], r.v1l[m], m)
+    def send_field_one(i):
+        remote(r.f1.at[i], level_rows(r.g1, at.i), r.s5, r.v5, at.w * 8 + i).start()
+
+    def wavenumber(k, carry):
+        m = (at.i + 1 + k) % 8
+        pl.when(k > 0)(lambda: send_field_one((at.i + k) % 8))
+        n = 8 * at.w + m + col
+        spec = nn(r.vt[m], r.leg_hi[m]) + nn(r.vt[m], r.leg_lo[m]) + nn(r.vl[m], r.leg_hi[m])
+        spec = jnp.where(n < M, spec, 0.0)
+        done = spec / damping(n, strength)
         for c in range(2):
-            r.f1[m, c] = spec[c * 8 : c * 8 + 8]
+            r.f1[m, c] = spec[c * 32 + 8 : c * 32 + 16]
+            r.out[:, :, m, c, :] = done[c * 32 : (c + 1) * 32].reshape(F, 8, M)
         return carry
 
-    lax.fori_loop(0, 8, field_one, 0)
-    for d, i, device in at.level():
-        remote(r.f1.at[i], level_rows(r.g1, at.i), r.s5, r.v5, device).start()
+    with jax.named_scope("fall"):
+        lax.fori_loop(0, 8, wavenumber, 0)
     own = pltpu.make_async_copy(r.f1.at[at.i], level_rows(r.g1, at.i), r.own_sem.at[0, 0])
     own.start()
-
-    def pair(q, carry):
-        for h in range(2):
-            m = 2 * q + h
-            n, spec = basis(r.vt[q, h * 64 : (h + 1) * 64, :], r.vl[q, h * 64 : (h + 1) * 64, :], m)
-            done = spec / damping(n, strength)
-            for c in range(2):
-                r.out[:, :, m, c, :] = done[c * 32 : (c + 1) * 32].reshape(F, 8, M)
-        return carry
-
-    lax.fori_loop(0, 4, pair, 0)
     own.wait()
     n = 8 * at.w + at.i + col
     row = lax.broadcasted_iota(jnp.int32, (64, 64), 0)
@@ -414,9 +404,9 @@
     xl=((512, 256), bf16), s_hi=((HALF, 256), bf16), s_lo=((HALF, 256), bf16), d_hi=((HALF, 256), bf16),
     d_lo=((HALF, 256), bf16), yh=((2, 64, 4, 4, 128), bf16), yc=((2, 64, 4, 2, 128), bf16),
     r2=((3, 4, 32, 4, 128), bf16), c2=((3, 4, 32, 2, 128), bf16), vr=((3, 4, 32, 4, 128), bf16),
-    vc=((3, 4, 32, 2, 128), bf16), vs=((1536, 128), f32), vcs=((768, 128), f32), vt=((4, 128, LAT), bf16),
-    vl=((4, 128, LAT), bf16), f1=((8, 2, 8, M), f32), g1=((2, 64, M), f32), hs=((2, 64, M), f32),
-    qs=((8, 2, 8, M), f32), v1t=((8, 16, LAT), bf16), v1l=((8, 16, LAT), bf16),
+    vc=((3, 4, 32, 2, 128), bf16), vs=((1536, 128), f32), vcs=((768, 128), f32), vt=((8, 64, LAT), bf16),
+    vl=((8, 64, LAT), bf16), f1=((8, 2, 8, M), f32), g1=((2, 64, M), f32), hs=((2, 64, M), f32),
+    qs=((8, 2, 8, M), f32),
 )
 SEMS = dict(
     leg_sem=(8,), load_sem=(8,), own_sem=(2, 2), lat_sem=(3,), y_own=(2, 3), s1=(2, 3), v1=(2, 3), s2=(2, 3), v2=(2, 2),
@@ -525,7 +515,7 @@
     return pl.pallas_call(
         step_kernel,
         name="step",
-        out_shape=jax.ShapeDtypeStruct((F, 8, 8, 2, M), f32),
+        out_shape=pltpu.VMEM((F, 8, 8, 2, M), f32),
         in_specs=[ANY, ANY, SMEM, VMEM, VMEM, SMEM, VMEM, ANY, VMEM, ANY, VMEM, ANY, VMEM, ANY, ANY, ANY, ANY],
         out_specs=VMEM,
         scratch_shapes=[pltpu.VMEM(*s) for s in SCRATCH.values()] + [DMA(s) if s else DMA for s in SEMS.values()],

time: 68.3 us -> 65.8 us (0.963)
  local copies, waits for them, and re-layouts: 2.02 us -> 0.8 us
  Pallas kernels: 66 us -> 64.9 us
    unnamed x1, local copies, waits for them, and re-layouts: 2.02 us -> 0.8 us
    pallas_call x1, Pallas kernels: 66 us -> 64.9 us  [body(): pl.pallas_call(step_kernel, name='step', out_shape=pltpu.VMEM((F, 8, 8, 2...]
where the time goes in v1:
time: 65.8 us; the launch traced here: 65.7 us
  Pallas kernels  64.9 us (99%)
  local copies, waits for them, and re-layouts  0.8 us (1%)
    pallas_call x1, Pallas kernels, body(): pl.pallas_call(step_kernel, name='step', out_shape=pltpu.VMEM((F, 8, 8, 2...  64.9 us

profile of v1, /device:TPU:2, one launch (start us, length us, event | category | flops | bytes accessed | tf_op | source)
XLA Modules:
  0.0 65.7 jit_solution(18307049491767113938)
XLA Ops:
  0.0 64.9 %step.1 = f32[4,8,8,2,256]{4,3,2,1,0:T(2,128)S(1)} custom-call(f32[4,8,8,2,256]{4,3,2,1,0:T(2,128)} %refs_0_.1, f32[8,384,256]{2,1,0:T(8,128)} %refs_1_.1, f32[12]{0:T(128)} %refs_2_.1, f32[64,64]{1,0:T(8,128)} %refs_3_.1, f32[1,64]{1,0:T(1,128)} %bitcast.9, f32[4]{0:T(128)} %refs_5_.1, f32[1,256]{1,0:T(1,128)} %bitcast.7, bf16[1024,256]{1,0:T(8,128)(2,1)} %refs_7_.1, ...), custom_call_target="tpu_custom_call" | custom-call | tf_op jit(solution)/shard_map/step/pallas_call | solution.py:515
  64.9 0.8 %copy.19 = f32[4,8,8,2,256]{4,3,2,1,0:T(2,128)} copy(f32[4,8,8,2,256]{4,3,2,1,0:T(2,128)S(1)} %step.1) | data formatting | bytes 1048576

commit v2 on v1

--- a/solution.py
+++ b/solution.py
@@ -35,15 +35,15 @@
     return hi, (x - hi.astype(f32)).astype(bf16)
 
 
-def encode(x):
+def encode(x, steps):
     hi = x.astype(bf16).astype(f32)
     size = jnp.abs(hi)
     r = jnp.where(size > 0.0, (x - hi) / size, 0.0)
-    return hi, jnp.clip(jnp.floor(r * 2048.0 + 8.0), 0.0, 15.0)
-
-
-def decode(hi, k):
-    return hi + jnp.abs(hi) * ((k - 7.5) * (1.0 / 2048.0))
+    return hi, jnp.clip(jnp.floor(r * (128.0 * steps) + 0.5 * steps), 0.0, steps - 1.0)
+
+
+def decode(hi, k, steps):
+    return hi + jnp.abs(hi) * ((k - (0.5 * steps - 0.5)) * (1.0 / (128.0 * steps)))
 
 
 def gelu(x):
@@ -152,7 +152,7 @@
     def pack(k, carry):
         code = []
         for q in range(4):
-            hi, step = encode(r.band[q, pl.ds(pl.multiple_of(24 * k, 8), 24), :])
+            hi, step = encode(r.band[q, pl.ds(pl.multiple_of(24 * k, 8), 24), :], 16)
             r.tmp[pl.ds(q, 24, stride=4), :] = hi
             code.append(step)
         r.tmc[pl.ds(0, 24, stride=2), :] = 16.0 * code[0] + code[1]
@@ -167,17 +167,22 @@
     lax.fori_loop(0, 16, pack, 0)
 
 
+def third(src, t, y):
+    return src.at[t, y] if src.shape[1] == 4 else src.at[t, y // 2]
+
+
 def along_y_start(at, t, pairs, send, recv, own_sem):
     for n, (src, dst) in enumerate(pairs):
         for d, y, device in at.column():
-            remote(src.at[t, y], dst.at[t, at.y], send.at[n, t], recv.at[n, t], device).start()
-        pltpu.make_async_copy(src.at[t, at.y], dst.at[t, at.y], own_sem.at[n, t]).start()
+            remote(third(src, t, y), dst.at[t, at.y], send.at[n, t], recv.at[n, t], device).start()
+        pltpu.make_async_copy(third(src, t, at.y), dst.at[t, at.y], own_sem.at[n, t]).start()
 
 
 def along_y_wait(at, t, pairs, send, recv, own_sem):
     for n, (src, dst) in enumerate(pairs):
-        remote(src.at[t, pl.ds(0, 3)], dst.at[t, pl.ds(0, 3)], send.at[n, t], recv.at[n, t], 0).wait()
-        pltpu.make_async_copy(src.at[t, at.y], dst.at[t, at.y], own_sem.at[n, t]).wait()
+        some = dst.at[t, pl.ds(0, 3)]
+        remote(some, some, send.at[n, t], recv.at[n, t], 0).wait()
+        pltpu.make_async_copy(third(src, t, at.y), dst.at[t, at.y], own_sem.at[n, t]).wait()
 
 
 def to_grid_start(at, r, t):
@@ -229,7 +234,7 @@
             first = jnp.floor(code * (1.0 / 16.0))
             r.steps[k, pl.ds(0, 64, stride=2), :] = first
             r.steps[k, pl.ds(1, 64, stride=2), :] = code - 16.0 * first
-            v.append(decode(r.xh.reshape(2, 32, 2, 4, 4, 128)[a, :, zl, y].astype(f32).reshape(128, 128), r.steps[k]))
+            v.append(decode(r.xh.reshape(2, 32, 2, 4, 4, 128)[a, :, zl, y].astype(f32).reshape(128, 128), r.steps[k], 16))
         for b, t in enumerate(block_transpose(v)):
             here = (slice(b * 128, (b + 1) * 128), slice(g * 128, (g + 1) * 128))
             r.xt[here], r.xl[here] = split(t)
@@ -239,7 +244,7 @@
         return nn(hi, x) + nn(lo, x) + nn(hi, rest)
 
     def columns(k, carry):
-        rows = pl.ds(pl.multiple_of(k * 128, 128), 128)
+        rows = pl.ds(pl.multiple_of(k * 192, 64), 192)
         even, odd = inverse(rows, slice(0, 256)), inverse(rows, slice(256, 512))
         grid = jnp.concatenate([even + odd, even - odd], axis=0)
         v = grid.astype(bf16).astype(f32)
@@ -249,11 +254,11 @@
         h = gelu(nt(h, r.w2v[...]) + r.b2[...]).astype(bf16)
         t = (nt(h, r.w3p[...]) + r.b3p[...]).astype(bf16)
         u = (grid + t.astype(f32)) * weight
-        r.s_hi[rows, :], r.s_lo[rows, :] = split(u[:128] + u[128:])
-        r.d_hi[rows, :], r.d_lo[rows, :] = split(u[:128] - u[128:])
+        r.s_hi[rows, :], r.s_lo[rows, :] = split(u[:192] + u[192:])
+        r.d_hi[rows, :], r.d_lo[rows, :] = split(u[:192] - u[192:])
         return carry
 
-    lax.fori_loop(0, 3, columns, 0)
+    lax.fori_loop(0, 2, columns, 0)
 
     def forward(half, hi, lo):
         return nn(r.fh[half, :], hi[...]) + nn(r.fh[half, :], lo[...]) + nn(r.fl[half, :], hi[...])
@@ -261,12 +266,16 @@
     even, odd = forward(slice(0, 256), r.s_hi, r.s_lo), forward(slice(256, 512), r.d_hi, r.d_lo)
     y = (even[:128], even[128:], odd[:128], odd[128:])
     for g in range(2):
+        code = []
         for k, t in enumerate(block_transpose([v[:, g * 128 : (g + 1) * 128] for v in y])):
-            hi, step = encode(t)
+            hi, step = encode(t, 4)
             r.steps[k] = step
-            code = 16.0 * r.steps[k, pl.ds(0, 64, stride=2), :] + r.steps[k, pl.ds(1, 64, stride=2), :]
+            rows = [r.steps[k, pl.ds(q, 32, stride=4), :] for q in range(4)]
+            code.append(64.0 * rows[0] + 16.0 * rows[1] + (4.0 * rows[2] + rows[3]))
             r.yh.reshape(2, 32, 2, 4, 4, 128)[a, :, k % 2, 2 * g + k // 2] = hi.reshape(32, 4, 128).astype(bf16)
-            r.yc.reshape(2, 32, 2, 4, 2, 128)[a, :, k % 2, 2 * g + k // 2] = code.reshape(32, 2, 128).astype(bf16)
+        for zl in range(2):
+            both = jnp.stack([code[zl], code[zl + 2]], axis=1)
+            r.yc.reshape(2, 32, 2, 2, 2, 128)[a, :, zl, g] = both.astype(bf16)
 
 
 def network_weights(r):
@@ -318,17 +327,18 @@
 def legendre_back(at, r):
     def unpack(k, carry):
         hi = jnp.stack([r.vr[t, :, pl.ds(2 * k, 2)].astype(f32) for t in range(3)], axis=2)
-        low = jnp.stack([r.vc[t, :, pl.ds(2 * k, 2)].astype(f32) for t in range(3)], axis=2)
+        tiles = [r.vc[t, :, pl.ds(2 * k, 2)].astype(f32) for t in range(3)]
+        low = jnp.stack([jnp.where(at.y % 2 == 0, v[:, :, 0], v[:, :, 1]) for v in tiles], axis=2)
         r.vs[pl.ds(pl.multiple_of(96 * k, 8), 96), :] = hi.reshape(96, 128)
-        r.vcs[pl.ds(pl.multiple_of(48 * k, 8), 48), :] = low.reshape(48, 128)
+        r.vcs[pl.ds(pl.multiple_of(24 * k, 8), 24), :] = low.reshape(24, 128)
         return carry
 
     lax.fori_loop(0, 16, unpack, 0)
-    for q in range(4):
-        code = r.vcs[pl.ds(q // 2, LAT, stride=2), :]
-        first = jnp.floor(code * (1.0 / 16.0))
-        step = first if q % 2 == 0 else code - 16.0 * first
-        turned = decode(r.vs[pl.ds(q, LAT, stride=4), :], step).T
+    rest = r.vcs[...]
+    for q, unit in enumerate((64.0, 16.0, 4.0, 1.0)):
+        step = jnp.floor(rest * (1.0 / unit))
+        rest = rest - unit * step
+        turned = decode(r.vs[pl.ds(q, LAT, stride=4), :], step, 4).T
         for h in range(2):
             r.vt[2 * q + h], r.vl[2 * q + h] = split(turned[h * 64 : (h + 1) * 64])
     col = lax.broadcasted_iota(jnp.int32, (64, M), 1)
@@ -402,9 +412,9 @@
     fh=((512, HALF), bf16), fl=((512, HALF), bf16), w1p=((HID, 256), bf16), w3p=((256, HID), bf16),
     gain_p=((1, 256), f32), b3p=((1, 256), f32), steps=((4, 128, 128), f32), xt=((512, 256), bf16),
     xl=((512, 256), bf16), s_hi=((HALF, 256), bf16), s_lo=((HALF, 256), bf16), d_hi=((HALF, 256), bf16),
-    d_lo=((HALF, 256), bf16), yh=((2, 64, 4, 4, 128), bf16), yc=((2, 64, 4, 2, 128), bf16),
-    r2=((3, 4, 32, 4, 128), bf16), c2=((3, 4, 32, 2, 128), bf16), vr=((3, 4, 32, 4, 128), bf16),
-    vc=((3, 4, 32, 2, 128), bf16), vs=((1536, 128), f32), vcs=((768, 128), f32), vt=((8, 64, LAT), bf16),
+    d_lo=((HALF, 256), bf16), yh=((2, 64, 4, 4, 128), bf16), yc=((2, 64, 2, 2, 128), bf16),
+    r2=((3, 4, 32, 4, 128), bf16), c2=((3, 2, 32, 2, 128), bf16), vr=((3, 4, 32, 4, 128), bf16),
+    vc=((3, 4, 32, 2, 128), bf16), vs=((1536, 128), f32), vcs=((LAT, 128), f32), vt=((8, 64, LAT), bf16),
     vl=((8, 64, LAT), bf16), f1=((8, 2, 8, M), f32), g1=((2, 64, M), f32), hs=((2, 64, M), f32),
     qs=((8, 2, 8, M), f32),
 )

time: 65.8 us -> 64.2 us (0.976)
  Pallas kernels: 64.9 us -> 63.2 us
    pallas_call x1, Pallas kernels: 64.9 us -> 63.2 us  [body(): pl.pallas_call(step_kernel, name='step', out_shape=pltpu.VMEM((F, 8, 8, 2...]
where the time goes in v2:
time: 64.2 us; the launch traced here: 64 us
  Pallas kernels  63.2 us (98%)
  local copies, waits for them, and re-layouts  0.8 us (1%)
    pallas_call x1, Pallas kernels, body(): pl.pallas_call(step_kernel, name='step', out_shape=pltpu.VMEM((F, 8, 8, 2...  63.2 us

profile of v2, /device:TPU:2, one launch (start us, length us, event | category | flops | bytes accessed | tf_op | source)
XLA Modules:
  0.0 64.0 jit_solution(11196300564019211119)
XLA Ops:
  0.0 63.2 %step.1 = f32[4,8,8,2,256]{4,3,2,1,0:T(2,128)S(1)} custom-call(f32[4,8,8,2,256]{4,3,2,1,0:T(2,128)} %refs_0_.1, f32[8,384,256]{2,1,0:T(8,128)} %refs_1_.1, f32[12]{0:T(128)} %refs_2_.1, f32[64,64]{1,0:T(8,128)} %refs_3_.1, f32[1,64]{1,0:T(1,128)} %bitcast.9, f32[4]{0:T(128)} %refs_5_.1, f32[1,256]{1,0:T(1,128)} %bitcast.7, bf16[1024,256]{1,0:T(8,128)(2,1)} %refs_7_.1, ...), custom_call_target="tpu_custom_call" | custom-call | tf_op jit(solution)/shard_map/step/pallas_call | solution.py:525
  63.2 0.8 %copy.19 = f32[4,8,8,2,256]{4,3,2,1,0:T(2,128)} copy(f32[4,8,8,2,256]{4,3,2,1,0:T(2,128)S(1)} %step.1) | data formatting | bytes 1048576
